TPU v7x, 128 devices: a whole 4x4x4 slice. The times are simulated.
128 devices in a mesh: branch: 2 (over core), dp: 8 (over x, z_hi), mp: 8 (over z_lo, y).
Axes of the slice: x: 4, y: 4, z: 4 (z_hi: 2, z_lo: 2; z = z_hi * 2 + z_lo), core: 2. Of those that a mesh axis runs over, the one named last changes fastest.
Arguments:
- unet_hidden: bfloat16 [16, 1280, 256], P(('branch', 'dp'), 'mp'), may hold values from -6 to 6
- control_hidden: bfloat16 [2, 2, 8, 1280, 256], P('branch', None, 'dp', 'mp'), may hold values from -6 to 6
- timesteps: int32 [2, 8], P(None, 'dp'), may hold values from 0 to 999
- control_scales: int32 [2, 2, 8], P('branch', None, 'dp'), may hold values from 1 to 16
- unet_time_first: bfloat16 [320, 1280], replicated, may hold values from -0.3125 to 0.3125
- unet_time_second: bfloat16 [1280, 1280], replicated, may hold values from -0.15625 to 0.15625
- unet_proj: bfloat16 [1280, 1280], P(None, 'mp'), may hold values from -0.15625 to 0.15625
- unet_conv_first: bfloat16 [9, 1280, 1280], P(None, 'mp'), may hold values from -0.0546875 to 0.0546875
- unet_conv_second: bfloat16 [9, 1280, 1280], P(None, 'mp'), may hold values from -0.0546875 to 0.0546875
- control_time_first: bfloat16 [2, 320, 1280], P('branch'), may hold values from -0.3125 to 0.3125
- control_time_second: bfloat16 [2, 1280, 1280], P('branch'), may hold values from -0.15625 to 0.15625
- control_proj: bfloat16 [2, 1280, 1280], P('branch', None, 'mp'), may hold values from -0.15625 to 0.15625
- control_conv_first: bfloat16 [2, 9, 1280, 1280], P('branch', None, 'mp'), may hold values from -0.0546875 to 0.0546875
- control_conv_second: bfloat16 [2, 9, 1280, 1280], P('branch', None, 'mp'), may hold values from -0.0546875 to 0.0546875
- zero_conv: bfloat16 [2, 1280, 1280], P('branch', 'mp'), may hold values from -0.15625 to 0.15625
Outputs:
- skip_out: bfloat16 [16, 1280, 256], P(('branch', 'dp'), 'mp')
All inputs are finite; a program needn't handle non-finite values.
Results may differ from a plain program's by a relative error of at most 0.018.
Values may be sent and summed in bfloat16 or wider, within the bound.
A program may use at most 128 MiB of HBM per device.

v0:
```python
import math

import jax
import jax.numpy as jnp
from jax import lax
from jax.sharding import PartitionSpec as P

C = 1280
TDIM = 320
GROUPS = 32
SIDE = 16


def joined_along(pieces, dim):
    pieces = jnp.moveaxis(pieces, 0, dim)
    shape = pieces.shape
    return pieces.reshape(*shape[:dim], shape[dim] * shape[dim + 1], *shape[dim + 2 :])


def copy_for_each(array, axis):
    copies = jnp.broadcast_to(array, (lax.axis_size(axis), *array.shape))
    return lax.all_to_all(copies, axis, split_axis=0, concat_axis=0, tiled=True)


def gathered_copies(array, axis, dim):
    return joined_along(copy_for_each(array, axis), dim)


def split_up(array, dim, peers):
    shape = array.shape
    pieces = array.reshape(*shape[:dim], peers, shape[dim] // peers, *shape[dim + 1 :])
    return jnp.moveaxis(pieces, dim, 0)


def sent_and_summed(array, axis, dim):
    peers = lax.axis_size(axis)
    pieces = lax.all_to_all(split_up(array, dim, peers), axis, 0, 0, tiled=True)
    return jnp.sum(pieces.astype(jnp.float32), axis=0)


def sinusoid(step_ids):
    half_width = TDIM // 2
    frequency = jnp.exp(-math.log(10000.0) * jnp.arange(half_width, dtype=jnp.float32) / half_width)
    angles = step_ids.astype(jnp.float32)[:, None] * frequency[None, :]
    return jnp.concatenate([jnp.cos(angles), jnp.sin(angles)], axis=1)


def time_embed(step_ids, first_weight, second_weight):
    waves = sinusoid(step_ids).astype(jnp.bfloat16)
    middle = jax.nn.silu(jnp.dot(waves, first_weight, preferred_element_type=jnp.float32)).astype(
        jnp.bfloat16
    )
    embedded = jnp.dot(middle, second_weight, preferred_element_type=jnp.float32)
    return jax.nn.silu(embedded).astype(jnp.bfloat16)


def norm_silu(values):
    image_count, width, pixels = values.shape
    group_size = C // GROUPS
    grouped = values.reshape(image_count, width // group_size, group_size, pixels)
    group_mean = jnp.mean(grouped, axis=(2, 3), keepdims=True)
    centered = grouped - group_mean
    group_var = jnp.mean(centered * centered, axis=(2, 3), keepdims=True)
    normed = centered * lax.rsqrt(group_var + 1e-05)
    return jax.nn.silu(normed).reshape(image_count, width, pixels)


def conv_taps(activation, weight, einsum_form):
    image_count, width, pixels = activation.shape
    image_grid = activation.reshape(image_count, width, SIDE, SIDE)
    padded = jnp.pad(image_grid, ((0, 0), (0, 0), (1, 1), (1, 1)))
    accum_sum = None
    for tap_index in range(9):
        row_shift = tap_index // 3
        col_shift = tap_index % 3
        window = padded[:, :, row_shift : row_shift + SIDE, col_shift : col_shift + SIDE].reshape(
            image_count, width, pixels
        )
        term = jnp.einsum(
            einsum_form, weight[tap_index], window, preferred_element_type=jnp.float32
        )
        accum_sum = term if accum_sum is None else accum_sum + term
    return accum_sum


def resnet_block(hidden, conv_first, conv_second, time_proj, time_act, for_unet):
    start_sum = jnp.zeros((hidden.shape[0], conv_first.shape[1], hidden.shape[2]), jnp.float32)
    start_sum = (
        start_sum + jnp.dot(time_act, time_proj, preferred_element_type=jnp.float32)[:, :, None]
    )
    operand = norm_silu(hidden.astype(jnp.float32)).astype(jnp.bfloat16)

    def fold_first(running, shard_piece):
        return running + conv_taps(shard_piece, conv_first, "oc,bcp->bop")

    if for_unet:
        inner_sum = fold_first(start_sum, gathered_copies(operand, "mp", 1))
    else:
        inner_sum = fold_first(start_sum, gathered_copies(operand, "mp", 1))
    second_act = norm_silu(inner_sum).astype(jnp.bfloat16)
    partial_sum = conv_taps(second_act, conv_second, "co,bcp->bop")
    if for_unet:
        outer_sum = sent_and_summed(partial_sum.astype(jnp.bfloat16), "mp", 1)
    else:
        outer_sum = sent_and_summed(partial_sum.astype(jnp.bfloat16), "mp", 1)
    return hidden.astype(jnp.float32) + outer_sum


def shards(
    unet_hidden,
    control_hidden,
    timesteps,
    control_scales,
    unet_time_first,
    unet_time_second,
    unet_proj,
    unet_conv_first,
    unet_conv_second,
    control_time_first,
    control_time_second,
    control_proj,
    control_conv_first,
    control_conv_second,
    zero_conv,
):
    model_ways = lax.axis_size("mp")
    halves, image_count = timesteps.shape
    local_width = unet_hidden.shape[1]
    pixels = unet_hidden.shape[2]
    own_steps = lax.dynamic_index_in_dim(timesteps, lax.axis_index("branch"), 0, keepdims=False)
    time_act = time_embed(own_steps, unet_time_first, unet_time_second)
    unet_out = resnet_block(
        unet_hidden, unet_conv_first, unet_conv_second, unet_proj, time_act, True
    )
    time_act = time_embed(
        timesteps.reshape(halves * image_count), control_time_first[0], control_time_second[0]
    )
    stacked = control_hidden[0].reshape(halves * image_count, local_width, pixels)
    copy_out = resnet_block(
        stacked, control_conv_first[0], control_conv_second[0], control_proj[0], time_act, False
    ).astype(jnp.bfloat16)
    weight_blocks = zero_conv[0].reshape(local_width, model_ways, local_width)
    shaped = copy_out.reshape(halves, image_count, local_width, pixels)
    zero_terms = jnp.einsum(
        "ckd,hbcp->hkbdp", weight_blocks, shaped, preferred_element_type=jnp.float32
    )
    scale_factor = control_scales[0].astype(jnp.float32) / 8.0
    zero_terms = zero_terms * scale_factor[:, None, :, None, None]
    merged = zero_terms.reshape(halves * model_ways, image_count, local_width, pixels)
    residual = sent_and_summed(merged.astype(jnp.bfloat16), ("branch", "mp"), 0)[0]
    return (unet_out + residual).astype(jnp.bfloat16)


def solution(mesh):
    in_specs = (
        P(("branch", "dp"), "mp", None),
        P("branch", None, "dp", "mp", None),
        P(None, "dp"),
        P("branch", None, "dp"),
        P(),
        P(),
        P(None, "mp"),
        P(None, "mp", None),
        P(None, "mp", None),
        P("branch", None, None),
        P("branch", None, None),
        P("branch", None, "mp"),
        P("branch", None, "mp", None),
        P("branch", None, "mp", None),
        P("branch", "mp", None),
    )
    out_specs = P(("branch", "dp"), "mp", None)
    return jax.shard_map(shards, mesh=mesh, in_specs=in_specs, out_specs=out_specs, check_vma=False)
```

profile of v0, /device:TPU:0, one launch (start us, length us, event | category | flops | bytes accessed | tf_op | source)
XLA Modules:
  0.0 135.8 jit_solution(14638931305041278830)
XLA Ops:
  4.9 6.1 %all-to-all-start = ((bf16[8,1,160,256]{3,2,1,0:T(8,128)(2,1)}), bf16[8,1,160,256]{3,2,1,0:T(8,128)(2,1)}, u32[]{:S(2)}, u32[]{:S(2)}) async-start(bf16[8,1,160,256]{3,2,1,0:T(8,128)(2,1)} %broadcast_in_dim.4), calls=%async_computation | async-start | bytes 1310720 | tf_op jit(solution)/shard_map/all_to_all | solution.py:22
  11.7 1.2 fusion.143
  13.7 1.4 %convolution_reduce_fusion.1 = f32[1280]{0:T(1024)S(1)} fusion(bf16[320,1]{0,1:T(2,128)(2,1)S(1)} %reshape.517, bf16[320,1280]{1,0:T(8,128)(2,1)} %param.19), kind=kOutput, calls=%fused_computation.64 | convolution fusion | flops 819200 | bytes 824960 | tf_op jit(solution)/shard_map/dot_general | solution.py:50
  18.4 1.4 %fusion.131 = bf16[2,1280]{1,0:T(2,128)(2,1)S(1)} fusion(bf16[1,320,1280]{2,1,0:T(8,128)(2,1)} %param.24, bf16[2,160]{1,0:T(2,128)(2,1)S(1)} %get-tuple-element.38, bf16[2,160]{1,0:T(2,128)(2,1)S(1)} %get-tuple-element.37), kind=kOutput, calls=%fused_computation.206 | convolution fusion | flops 1653760 | bytes 825600 | tf_op jit(solution)/shard_map/dot_general | solution.py:50
  19.8 2.7 %fusion.33 = f32[2,160]{1,0:T(2,128)S(1)} fusion(bf16[1,1280,160]{1,2,0:T(8,128)(2,1)} %param.26, bf16[2,1280]{1,0:T(2,128)(2,1)S(1)} %fusion.131, bf16[1,1280,1280]{2,1,0:T(8,128)(2,1)} %param.25), kind=kOutput, calls=%fused_computation.99 | convolution fusion | flops 7385600 | bytes 3692800 | tf_op jit(solution)/shard_map/dot_general | solution.py:89
  22.6 1.2 broadcast_in_dim.5
  23.8 5.7 %all-to-all-start.2 = ((bf16[8,2,160,256]{3,2,1,0:T(8,128)(2,1)}), bf16[8,2,160,256]{3,2,1,0:T(8,128)(2,1)S(1)}, u32[]{:S(2)}, u32[]{:S(2)}) async-start(bf16[8,2,160,256]{3,2,1,0:T(8,128)(2,1)} %broadcast_in_dim.5), calls=%async_computation.2 | async-start | bytes 2621440 | tf_op jit(solution)/shard_map/all_to_all | solution.py:22
  29.5 1.8 %copy.96 = bf16[8,1,160,256]{2,0,3,1:T(8,128)(2,1)S(1)} copy(bf16[8,1,160,256]{3,2,1,0:T(8,128)(2,1)} %all-to-all-done) | data formatting | bytes 1310720 | tf_op jit(solution)/shard_map/all_to_all | solution.py:22
  32.5 1.5 %pad_slice_fusion.8 = (bf16[1,1280,16,16]{1,3,2,0:T(8,128)(2,1)S(1)}, bf16[1,1280,16,16]{1,3,2,0:T(8,128)(2,1)S(1)}, bf16[1,1280,16,16]{1,3,2,0:T(8,128)(2,1)S(1...) fusion(bf16[1,1280,16,16]{1,3,2,0:T(8,128)(2,1)S(1)} %reshape_r, ...), kind=kLoop, calls=%fused_computation.34 | loop fusion | bytes 5898240 | tf_op jit(solution)/shard_map/slice | solution.py:76
  36.0 1.4 %convolution_add_fusion.24 = f32[256,160]{0,1:T(8,128)S(1)} fusion(f32[256,160]{0,1:T(8,128)S(1)} %convolution_add_fusion.29, bf16[1280,256]{1,0:T(8,128)(2,1)} %bitcast.11, bf16[9,160,1280]{2,1,0:T(8,128)(2,1)S(1)} %copy-done.6), kind=kOutput, calls=%fused_computation.53 | convolution fusion | flops 104898560 | bytes 1392640 | tf_op jit(solution)/shard_map/oc,bcp->bop/dot_general | solution.py:79
  41.2 1.3 fusion.43
  42.5 1.3 convolution_add_fusion.15
  43.8 1.3 convolution_add_fusion.14
  45.2 2.4 %convolution_add_fusion.13 = f32[256,1280]{1,0:T(8,128)} fusion(f32[256,1280]{1,0:T(8,128)S(1)} %convolution_add_fusion.14, bf16[160,256]{0,1:T(8,128)(2,1)S(1)} %bitcast.389, bf16[9,160,1280]{2,1,0:T(8,128)(2,1)} %param.23), kind=kOutput, calls=%fused_computation.24 | convolution fusion | flops 105185280 | bytes 3112960 | tf_op jit(solution)/shard_map/co,bcp->bop/dot_general | solution.py:79
  47.6 1.9 %copy.101 = bf16[2,8,160,256]{2,1,3,0:T(8,128)(2,1)S(1)} copy(bf16[2,8,160,256]{3,2,0,1:T(8,128)(2,1)S(1)} %bitcast.353) | data formatting | bytes 2621440 | tf_op jit(solution)/shard_map/transpose | solution.py:15
  50.6 2.4 %reshape_reshape.3 = bf16[2,1280,16,16]{1,3,2,0:T(8,128)(2,1)S(1)} reshape(bf16[2,8,160,256]{2,1,3,0:T(8,128)(2,1)S(1)} %copy.101) | data formatting | bytes 2621440 | tf_op jit(solution)/shard_map/reshape;reshape | solution.py:70
  53.0 3.2 %pad_slice_fusion = (bf16[2,1280,16,16]{1,3,2,0:T(8,128)(2,1)S(1)}, bf16[2,1280,16,16]{1,3,2,0:T(8,128)(2,1)S(1)}, bf16[2,1280,16,16]{1,3,2,0:T(8,128)(2,1)S(1)}...) fusion(bf16[2,1280,16,16]{1,3,2,0:T(8,128)(2,1)S(1)} %reshape_r, ...), kind=kLoop, calls=%fused_computation | loop fusion | bytes 11796480 | tf_op jit(solution)/shard_map/slice | solution.py:76
  63.1 1.6 %fusion.21 = f32[2,256,1280]{2,1,0:T(8,128)S(1)} fusion(bf16[2,160,256]{1,2,0:T(8,128)(2,1)S(1)} %bitcast.382, bf16[1,9,160,1280]{3,2,1,0:T(8,128)(2,1)} %param.28), kind=kOutput, calls=%fused_computation.87 | convolution fusion | flops 209715200 | bytes 3194880 | tf_op jit(solution)/shard_map/co,bcp->bop/dot_general | solution.py:79
  70.8 5.8 %all-to-all-start.3 = ((bf16[8,2,160,256]{3,2,1,0:T(8,128)(2,1)}), bf16[8,2,160,256]{3,2,1,0:T(8,128)(2,1)S(1)}, u32[]{:S(2)}, u32[]{:S(2)}) async-start(bf16[8,2,160,256]{3,2,1,0:T(8,128)(2,1)} %copy.121), calls=%async_computation.3 | async-start | bytes 2621440 | tf_op jit(solution)/shard_map/all_to_all | solution.py:37
  76.6 1.4 %convolution_add_fusion.12 = f32[256,1280]{1,0:T(8,128)S(1)} fusion(f32[256,1280]{1,0:T(8,128)S(1)} %copy-done.2, bf16[9,160,1280]{2,1,0:T(8,128)(2,1)} %param.23, bf16[1,160,256]{2,1,0:T(8,128)(2,1)S(1)} %fusion.119), kind=kOutput, calls=%fused_computation.23 | convolution fusion | flops 105185280 | bytes 3112960 | tf_op jit(solution)/shard_map/co,bcp->bop/dot_general | solution.py:79
  78.1 1.4 convolution_add_fusion.11
  79.5 1.4 convolution_add_fusion.10
  80.8 1.3 convolution_add_fusion.9
  82.2 1.4 %fusion.6 = bf16[1,1280,256]{1,2,0:T(8,128)(2,1)S(1)} fusion(f32[256,1280]{1,0:T(8,128)S(1)} %convolution_add_fusion.9, bf16[160,256]{0,1:T(8,128)(2,1)S(1)} %bitcast.385, bf16[9,160,1280]{2,1,0:T(8,128)(2,1)} %param.23), kind=kOutput, calls=%fused_computation.33 | convolution fusion | flops 105512960 | bytes 2457600 | tf_op jit(solution)/shard_map/co,bcp->bop/dot_general | solution.py:79
  84.7 9.3 %all-to-all-done.3 = bf16[8,2,160,256]{3,2,1,0:T(8,128)(2,1)S(1)} async-done(((bf16[8,2,160,256]{3,2,1,0:T(8,128)(2,1)}), bf16[8,2,160,256]{3,2,1,0:T(8,128)(2,1)S(1)}, u32[]{:S(2)}, u32[]{:S(2)}) %all-to-all-start.3) | async-done | bytes 1310752 | tf_op jit(solution)/shard_map/all_to_all | solution.py:37
  94.0 4.2 %all-to-all-start.1 = ((bf16[8,1,160,256]{3,2,1,0:T(8,128)(2,1)}), bf16[8,1,160,256]{3,2,1,0:T(8,128)(2,1)}, u32[]{:S(2)}, u32[]{:S(2)}) async-start(bf16[8,1,160,256]{3,2,1,0:T(8,128)(2,1)} %bitcast.45), calls=%async_computation.1 | async-start | bytes 1310720 | tf_op jit(solution)/shard_map/all_to_all | solution.py:37
  98.7 1.6 %fusion.4 = bf16[2,1,256,8,160]{2,4,3,0,1:T(8,128)(2,1)} fusion(bf16[160,8,160,1]{0,2,1,3:T(8,128)(2,1)S(1)} %bitcast.366, f32[2]{0:T(128)S(1)} %multiply_bitcast_fusion, f32[2,160,256]{2,1,0:T(8,128)S(1)} %convert_reduce_fusion.1, bf16[1,2,1,160,256]{4,3,2,1,0:T(8,128)(2,1)S(1)} %copy-done.8), kind=kOutput, calls=%fused_computation.29 | convolution fusion | flops 211271680 | bytes 2211848 | tf_op jit(solution)/shard_map/ckd,hbcp->hkbdp/dot_general | solution.py:144
  100.3 9.6 %all-to-all-done.1 = bf16[8,1,160,256]{3,2,1,0:T(8,128)(2,1)} async-done(((bf16[8,1,160,256]{3,2,1,0:T(8,128)(2,1)}), bf16[8,1,160,256]{3,2,1,0:T(8,128)(2,1)}, u32[]{:S(2)}, u32[]{:S(2)}) %all-to-all-start.1) | async-done | bytes 655392 | tf_op jit(solution)/shard_map/all_to_all | solution.py:37
  109.9 4.6 %all-to-all-start.4 = ((bf16[16,1,1,160,256]{4,3,2,1,0:T(8,128)(2,1)}), bf16[16,1,1,160,256]{4,3,2,1,0:T(8,128)(2,1)}, u32[]{:S(2)}, u32[]{:S(2)}) async-start(bf16[16,1,1,160,256]{4,3,2,1,0:T(8,128)(2,1)} %bitcast.356), calls=%async_computation.4 | async-start | bytes 2621440 | tf_op jit(solution)/shard_map/all_to_all | solution.py:37
  114.6 1.2 convert_reduce_fusion.2
  115.8 17.9 %all-to-all-done.4 = bf16[16,1,1,160,256]{4,3,2,1,0:T(8,128)(2,1)} async-done(((bf16[16,1,1,160,256]{4,3,2,1,0:T(8,128)(2,1)}), bf16[16,1,1,160,256]{4,3,2,1,0:T(8,128)(2,1)}, u32[]{:S(2)}, u32[]{:S(2)}) %all-to-all-start.4) | async-done | bytes 1310752 | tf_op jit(solution)/shard_map/all_to_all | solution.py:37
  133.7 1.5 %convert_reduce_fusion = f32[160,256]{1,0:T(8,128)S(1)} fusion(bf16[16,1,1,160,256]{4,3,2,1,0:T(8,128)(2,1)} %all-to-all-done.4), kind=kLoop, calls=%fused_computation.30 | loop fusion | flops 1269760 | bytes 1474560 | tf_op jit(solution)/shard_map/reduce_sum | solution.py:38
  (135 shorter events, 32.8 us)
Async XLA Ops:
  0.0 15.1 %copy-start = (bf16[1280,1280]{1,0:T(8,128)(2,1)S(1)}, bf16[1280,1280]{1,0:T(8,128)(2,1)}, u32[]{:S(2)}) copy-start(bf16[1280,1280]{1,0:T(8,128)(2,1)} %param.20) | copy-start | bytes 9830404
  4.9 10.8 %copy-start.7 = (bf16[1,2,1,160,256]{4,3,2,1,0:T(8,128)(2,1)S(1)}, bf16[1,2,1,160,256]{4,3,2,1,0:T(8,128)(2,1)}, u32[]{:S(2)}) copy-start(bf16[1,2,1,160,256]{4,3,2,1,0:T(8,128)(2,1)} %param.16) | copy-start | bytes 491524
  4.9 17.6 %all-to-all-start = ((bf16[8,1,160,256]{3,2,1,0:T(8,128)(2,1)}), bf16[8,1,160,256]{3,2,1,0:T(8,128)(2,1)}, u32[]{:S(2)}, u32[]{:S(2)}) async-start(bf16[8,1,160,256]{3,2,1,0:T(8,128)(2,1)} %broadcast_in_dim.4), calls=%async_computation | async-start | bytes 1310720 | tf_op jit(solution)/shard_map/all_to_all | solution.py:22
  23.8 23.8 %all-to-all-start.2 = ((bf16[8,2,160,256]{3,2,1,0:T(8,128)(2,1)}), bf16[8,2,160,256]{3,2,1,0:T(8,128)(2,1)S(1)}, u32[]{:S(2)}, u32[]{:S(2)}) async-start(bf16[8,2,160,256]{3,2,1,0:T(8,128)(2,1)} %broadcast_in_dim.5), calls=%async_computation.2 | async-start | bytes 2621440 | tf_op jit(solution)/shard_map/all_to_all | solution.py:22
  32.5 2.0 %copy-start.6 = (bf16[9,160,1280]{2,1,0:T(8,128)(2,1)S(1)}, bf16[9,160,1280]{2,1,0:T(8,128)(2,1)}, u32[]{:S(2)}) copy-start(bf16[9,160,1280]{2,1,0:T(8,128)(2,1)} %param.22) | copy-start | bytes 11059204
  53.0 3.2 %copy-start.5 = (bf16[1,9,160,1280]{3,2,1,0:T(8,128)(2,1)S(1)}, bf16[1,9,160,1280]{3,2,1,0:T(8,128)(2,1)}, u32[]{:S(2)}) copy-start(bf16[1,9,160,1280]{3,2,1,0:T(8,128)(2,1)} %param.27) | copy-start | bytes 11059204
  57.4 1.3 copy-start.3
  62.8 2.2 %copy-start.4 = (bf16[1,9,160,1280]{3,2,1,0:T(8,128)(2,1)S(1)}, bf16[1,9,160,1280]{3,2,1,0:T(8,128)(2,1)}, u32[]{:S(2)}) copy-start(bf16[1,9,160,1280]{3,2,1,0:T(8,128)(2,1)} %param.28) | copy-start | bytes 11059204
  69.7 7.0 %copy-start.2 = (f32[256,1280]{1,0:T(8,128)S(1)}, f32[256,1280]{1,0:T(8,128)}, u32[]{:S(2)}) copy-start(f32[256,1280]{1,0:T(8,128)} %convolution_add_fusion.13) | copy-start | bytes 3932164
  70.8 7.2 %copy-start.13 = (bf16[1,160,16,16]{1,3,2,0:T(8,128)(2,1)S(1)}, bf16[1,160,16,16]{1,3,2,0:T(8,128)(2,1)}, u32[]{:S(2)}) copy-start(bf16[1,160,16,16]{1,3,2,0:T(8,128)(2,1)} %get-tuple-element.33) | copy-start | bytes 245764
  70.8 23.2 %all-to-all-start.3 = ((bf16[8,2,160,256]{3,2,1,0:T(8,128)(2,1)}), bf16[8,2,160,256]{3,2,1,0:T(8,128)(2,1)S(1)}, u32[]{:S(2)}, u32[]{:S(2)}) async-start(bf16[8,2,160,256]{3,2,1,0:T(8,128)(2,1)} %copy.121), calls=%async_computation.3 | async-start | bytes 2621440 | tf_op jit(solution)/shard_map/all_to_all | solution.py:37
  76.6 2.8 %copy-start.12 = (bf16[1,160,16,16]{1,3,2,0:T(8,128)(2,1)S(1)}, bf16[1,160,16,16]{1,3,2,0:T(8,128)(2,1)}, u32[]{:S(2)}) copy-start(bf16[1,160,16,16]{1,3,2,0:T(8,128)(2,1)} %get-tuple-element.34) | copy-start | bytes 245764
  78.1 2.8 %copy-start.11 = (bf16[1,160,16,16]{1,3,2,0:T(8,128)(2,1)S(1)}, bf16[1,160,16,16]{1,3,2,0:T(8,128)(2,1)}, u32[]{:S(2)}) copy-start(bf16[1,160,16,16]{1,3,2,0:T(8,128)(2,1)} %get-tuple-element.35) | copy-start | bytes 245764
  79.4 2.7 %copy-start.10 = (bf16[1,160,16,16]{1,3,2,0:T(8,128)(2,1)S(1)}, bf16[1,160,16,16]{1,3,2,0:T(8,128)(2,1)}, u32[]{:S(2)}) copy-start(bf16[1,160,16,16]{1,3,2,0:T(8,128)(2,1)} %get-tuple-element.29) | copy-start | bytes 245764
  82.2 16.1 %copy-start.15 = (s32[1,2,1]{1,2,0:T(1,128)S(1)}, s32[1,2,1]{1,2,0:T(1,128)}, u32[]{:S(2)}) copy-start(s32[1,2,1]{1,2,0:T(1,128)} %param.18) | copy-start | bytes 28
  82.2 16.1 %copy-start.14 = (bf16[1,160,1280]{2,1,0:T(8,128)(2,1)S(1)}, bf16[1,160,1280]{2,1,0:T(8,128)(2,1)}, u32[]{:S(2)}) copy-start(bf16[1,160,1280]{2,1,0:T(8,128)(2,1)} %param.29) | copy-start | bytes 1228804
  83.6 15.1 %copy-start.8 = (bf16[1,2,1,160,256]{4,3,2,1,0:T(8,128)(2,1)S(1)}, bf16[1,2,1,160,256]{4,3,2,1,0:T(8,128)(2,1)}, u32[]{:S(2)}) copy-start(bf16[1,2,1,160,256]{4,3,2,1,0:T(8,128)(2,1)} %param.16) | copy-start | bytes 491524
  94.0 15.9 %all-to-all-start.1 = ((bf16[8,1,160,256]{3,2,1,0:T(8,128)(2,1)}), bf16[8,1,160,256]{3,2,1,0:T(8,128)(2,1)}, u32[]{:S(2)}, u32[]{:S(2)}) async-start(bf16[8,1,160,256]{3,2,1,0:T(8,128)(2,1)} %bitcast.45), calls=%async_computation.1 | async-start | bytes 1310720 | tf_op jit(solution)/shard_map/all_to_all | solution.py:37
  100.3 34.9 %copy-start.9 = (bf16[1,160,256]{2,1,0:T(8,128)(2,1)S(1)}, bf16[1,160,256]{2,1,0:T(8,128)(2,1)}, u32[]{:S(2)}) copy-start(bf16[1,160,256]{2,1,0:T(8,128)(2,1)} %param.15) | copy-start | bytes 245764
  109.9 25.9 %copy-start.1 = (bf16[1280,1280]{1,0:T(8,128)(2,1)S(1)}, bf16[1280,1280]{1,0:T(8,128)(2,1)}, u32[]{:S(2)}) copy-start(bf16[1280,1280]{1,0:T(8,128)(2,1)} %param.20) | copy-start | bytes 9830404
  109.9 23.7 %all-to-all-start.4 = ((bf16[16,1,1,160,256]{4,3,2,1,0:T(8,128)(2,1)}), bf16[16,1,1,160,256]{4,3,2,1,0:T(8,128)(2,1)}, u32[]{:S(2)}, u32[]{:S(2)}) async-start(bf16[16,1,1,160,256]{4,3,2,1,0:T(8,128)(2,1)} %bitcast.356), calls=%async_computation.4 | async-start | bytes 2621440 | tf_op jit(solution)/shard_map/all_to_all | solution.py:37
where the time goes:
time: 138 us; the launch traced here: 136 us
  matrix products  37.3 us (27%)
  waiting for transfers between devices  36.9 us (27%)
  starting transfers between devices  26.4 us (19%)
  local copies, waits for them, and re-layouts  22.6 us (16%)
  other arithmetic  12 us (9%)
    all_to_all x3, waiting for transfers between devices, sent_and_summed(): pieces = lax.all_to_all(split_up(array, dim, peers), axis, 0, 0, tiled=True)  36.9 us
    dot_general x36, matrix products, conv_taps(): jnp.einsum(einsum_form, weight[tap_index], window, preferred_element_type...  28.5 us
    all_to_all x3, starting transfers between devices, sent_and_summed(): pieces = lax.all_to_all(split_up(array, dim, peers), axis, 0, 0, tiled=True)  14.7 us
    all_to_all x2, starting transfers between devices, copy_for_each(): return lax.all_to_all(copies, axis, split_axis=0, concat_axis=0, tiled=True)  11.8 us
    slice x4, local copies, waits for them, and re-layouts, conv_taps(): padded[:, :, row_shift:row_shift + SIDE, col_shift:col_shift + SIDE]  5.82 us
    dot_general x2, matrix products, resnet_block(): jnp.dot(time_act, time_proj, preferred_element_type=jnp.float32)[:, :, None]  3.9 us
    another operation x2, local copies, waits for them, and re-layouts, conv_taps(): image_grid = activation.reshape(image_count, width, SIDE, SIDE)  3.53 us
    transpose x2, local copies, waits for them, and re-layouts, joined_along(): pieces = jnp.moveaxis(pieces, 0, dim)  3.01 us
  transfers between devices with their start and end apart: 5, of which 3 were waited for; matrix products, arithmetic and copies ran while one was open for 29% of the time, Pallas kernels for 0%

commit v1 on v0

v1 whole, which is shorter than its diff:
```python
import functools
import math

import jax
import jax.numpy as jnp
from jax import lax
from jax.experimental import pallas as pl
from jax.experimental.pallas import tpu as pltpu
from jax.sharding import PartitionSpec as P

C = 1280
TDIM = 320
SIDE = 16
PIX = 256
WIDTH = 160
GROUP = 40
HALF = 80
TAPS = 9
KPAD = 1536
ZPAD = 256
PARTS = 2
LANES = PIX // PARTS
MESH = pl.DeviceIdType.MESH
F32 = jnp.float32
BF16 = jnp.bfloat16


def silu(v):
    return v * 0.5 * (1.0 + jnp.tanh(v * 0.5))


def norm_silu(values):
    grouped = values.reshape(WIDTH // GROUP, GROUP, PIX)
    scale = 1.0 / (GROUP * PIX)
    mean = jnp.sum(jnp.sum(grouped, axis=1, keepdims=True), axis=2, keepdims=True) * scale
    centered = grouped - mean
    var = jnp.sum(jnp.sum(centered * centered, axis=1, keepdims=True), axis=2, keepdims=True) * scale
    return silu(centered * lax.rsqrt(var + 1e-05)).reshape(WIDTH, PIX)


def shifted(values, step, pixel):
    return pltpu.roll(values, (-step) % PIX, 1)


def kernel(
    ts_ref, sc_ref, uh, ch, utf, uts, upr, uc1, uc2, ctf, cts, cpr, cc1, cc2, zc,
    out_ref,
    hid, act, w1, w2, w2t, tf, tw, pr, zw, zt, tpt, inner, shifts, part, co, zs, zr,
    st1, st2, st3, r1, r2, r3,
    load_sem, ag_send, ag_recv, s1, s2, s3, v1, v2, v3, swap_send, swap_recv,
):
    branch = lax.axis_index("branch")
    spot = lax.axis_index("mp")
    z = spot // 4
    y = spot % 4
    zo = 1 - z
    yp, ym, y2 = (y + 1) % 4, (y + 3) % 4, (y + 2) % 4
    up = {"mp": z * 4 + yp}
    down = {"mp": z * 4 + ym}
    across = {"mp": zo * 4 + y}
    partner = {"branch": 1 - branch}
    columns = (y2, yp, ym, y)

    sent = []

    def send(src, dst, ssem, rsem, target):
        copy = pltpu.make_async_remote_copy(
            src_ref=src, dst_ref=dst, send_sem=ssem, recv_sem=rsem, device_id=target, device_id_type=MESH
        )
        copy.start()
        sent.append(copy)

    def arrived(dst, rsem, ssem):
        pltpu.make_async_remote_copy(
            src_ref=dst, dst_ref=dst, send_sem=ssem, recv_sem=rsem, device_id=up, device_id_type=MESH
        ).wait_recv()

    barrier = pltpu.get_barrier_semaphore()
    for target in (up, down, across, partner):
        pl.semaphore_signal(barrier, inc=1, device_id=target, device_id_type=MESH)

    loads = {}

    def load(name, src, dst):
        loads[name] = pltpu.make_async_copy(src, dst, load_sem.at[len(loads)])
        loads[name].start()

    load("h0", ch.at[1 - branch], hid.at[0])
    load("h1", ch.at[branch], hid.at[1])
    load("h2", uh, hid.at[2])
    load("ctf", ctf, tf.at[0])
    load("cts", cts, tw.at[0])
    load("cpr", cpr, pr.at[0])
    load("cc1", cc1, w1.at[0])
    load("cc2", cc2, w2.at[0, pl.ds(0, TAPS * WIDTH)])
    load("utf", utf, tf.at[1])
    load("uts", uts, tw.at[1])
    load("upr", upr, pr.at[1])
    load("zc", zc, zw.at[pl.ds(0, WIDTH)])
    load("uc1", uc1, w1.at[1])
    load("uc2", uc2, w2.at[1, pl.ds(0, TAPS * WIDTH)])

    def rows(zz, yy):
        return pl.multiple_of((zz * 4 + yy) * WIDTH, 32)

    def piece(i, zz, yy, start=0, size=WIDTH):
        return act.at[i, pl.ds(pl.multiple_of(rows(zz, yy) + start, 16), size)]

    def normed(i, name):
        loads[name].wait()
        act[i, pl.ds(rows(z, y), WIDTH), :] = norm_silu(hid[i].astype(F32)).astype(BF16)

    def ag_own(i):
        own = piece(i, z, y)
        send(own, own, ag_send.at[i, 0], ag_recv.at[i, 0], across)
        send(own, own, ag_send.at[i, 1], ag_recv.at[i, 1], up)
        send(own, own, ag_send.at[i, 2], ag_recv.at[i, 2], down)

    def ag_a(i):
        got = piece(i, zo, y)
        arrived(got, ag_recv.at[i, 0], ag_send.at[i, 0])
        send(got, got, ag_send.at[i, 3], ag_recv.at[i, 3], up)
        send(got, got, ag_send.at[i, 4], ag_recv.at[i, 4], down)

    def ag_relay(i, zz, first, second):
        arrived(piece(i, zz, ym), ag_recv.at[i, first], ag_send.at[i, first])
        low = piece(i, zz, ym, 0, HALF)
        send(low, low, ag_send.at[i, second], ag_recv.at[i, second], up)
        arrived(piece(i, zz, yp), ag_recv.at[i, first + 1], ag_send.at[i, first + 1])
        high = piece(i, zz, yp, HALF, HALF)
        send(high, high, ag_send.at[i, second + 1], ag_recv.at[i, second + 1], down)

    def ag_b(i):
        ag_relay(i, z, 1, 5)

    def ag_c(i):
        ag_relay(i, zo, 3, 7)

    def ag_done(i):
        for zz, first in ((z, 5), (zo, 7)):
            arrived(piece(i, zz, y2, 0, HALF), ag_recv.at[i, first], ag_send.at[i, first])
            arrived(piece(i, zz, y2, HALF, HALF), ag_recv.at[i, first + 1], ag_send.at[i, first + 1])

    pixel = lax.broadcasted_iota(jnp.int32, (1, PIX), 1)
    column = pixel % SIDE
    not_left, not_right = column >= 1, column <= SIDE - 2
    not_top, not_bottom = pixel >= SIDE, pixel < PIX - SIDE

    def waves():
        lane = lax.broadcasted_iota(jnp.int32, (16, TDIM), 1)
        row = lax.broadcasted_iota(jnp.int32, (16, TDIM), 0)
        half_width = TDIM // 2
        index = jnp.where(lane < half_width, lane, lane - half_width).astype(F32)
        frequency = jnp.exp(-math.log(10000.0) * index / half_width)
        step = jnp.where(row == 0, ts_ref[0, 0].astype(F32), ts_ref[1, 0].astype(F32))
        angle = step * frequency
        return jnp.where(lane < half_width, jnp.cos(angle), jnp.sin(angle)).astype(BF16)

    def embed(k, first, second, third):
        loads[first].wait()
        middle = silu(jnp.dot(waves(), tf[k], preferred_element_type=F32)).astype(BF16)
        loads[second].wait()
        time_act = silu(jnp.dot(middle, tw[k], preferred_element_type=F32)).astype(BF16)
        loads[third].wait()
        projected = jnp.dot(time_act, pr[k], preferred_element_type=F32)
        wide = jnp.concatenate([projected, jnp.zeros((16, ZPAD - WIDTH), F32)], axis=1)
        tall = jnp.concatenate([wide, jnp.zeros((128 - 16, ZPAD), F32)], axis=0)
        tpt[k] = tall.T

    def time_column(k, half):
        lane = lax.broadcasted_iota(jnp.int32, (WIDTH, 128), 1)
        return jnp.sum(jnp.where(lane == half, tpt[k, 0:WIDTH, :], 0.0), axis=1, keepdims=True)

    def turned(src, dst):
        def body(j, carry):
            at = pl.multiple_of(j * 128, 128)
            dst[pl.ds(at, 128), :] = src[:, pl.ds(at, 128)].T
            return carry

        lax.fori_loop(0, C // 128, body, 0)

    def conv_first(i, k, dy):
        product = jnp.dot(
            w1[k, dy * 3 * WIDTH : (dy + 1) * 3 * WIDTH, :], act[i], preferred_element_type=F32
        )
        left = jnp.where(not_left, shifted(product[0:WIDTH], -1, pixel), 0.0)
        right = jnp.where(not_right, shifted(product[2 * WIDTH : 3 * WIDTH], 1, pixel), 0.0)
        total = left + product[WIDTH : 2 * WIDTH] + right
        if dy == 0:
            inner[...] = jnp.where(not_top, shifted(total, -SIDE, pixel), 0.0)
        elif dy == 1:
            inner[...] += total
        else:
            inner[...] += jnp.where(not_bottom, shifted(total, SIDE, pixel), 0.0)

    def second_operand(k, half):
        second = norm_silu(inner[...] + time_column(k, half))
        left = jnp.where(not_left, shifted(second, -1, pixel), 0.0)
        right = jnp.where(not_right, shifted(second, 1, pixel), 0.0)
        for dx, value in enumerate((left, second, right)):
            top = jnp.where(not_top, shifted(value, -SIDE, pixel), 0.0)
            bottom = jnp.where(not_bottom, shifted(value, SIDE, pixel), 0.0)
            for dy, moved in enumerate((top, value, bottom)):
                at = (dy * 3 + dx) * WIDTH
                shifts[at : at + WIDTH, :] = moved.astype(BF16)

    def both_planes(ref, yy):
        return jnp.concatenate([ref[pl.ds(rows(0, yy), WIDTH), :], ref[pl.ds(rows(1, yy), WIDTH), :]], axis=0)

    def conv_second(i, k, c):
        product = jnp.dot(both_planes(w2t.at[k], columns[c]), shifts[...], preferred_element_type=F32)
        part[i, c] = product.reshape(2, WIDTH, PIX)

    def lanes(h):
        return slice(h * LANES, (h + 1) * LANES)

    def rs1(i, h):
        st1[i, h] = part[i, 0, :, :, lanes(h)].astype(BF16)
        send(st1.at[i, h, :, pl.ds(0, HALF)], r1.at[i, h, 0], s1.at[i, h, 0], v1.at[i, h, 0], up)
        send(st1.at[i, h, :, pl.ds(HALF, HALF)], r1.at[i, h, 1], s1.at[i, h, 1], v1.at[i, h, 1], down)

    def rs2(i, h):
        for side, target in ((0, up), (1, down)):
            arrived(r1.at[i, h, side], v1.at[i, h, side], s1.at[i, h, side])
            plus = slice(side * HALF, (side + 1) * HALF)
            other = slice((1 - side) * HALF, (2 - side) * HALF)
            st2[i, h, side, :, plus, :] = (
                part[i, 1 + side, :, plus, lanes(h)] + r1[i, h, side].astype(F32)
            ).astype(BF16)
            st2[i, h, side, :, other, :] = part[i, 1 + side, :, other, lanes(h)].astype(BF16)
            send(st2.at[i, h, side], r2.at[i, h, side], s2.at[i, h, side], v2.at[i, h, side], target)

    def column_sum(i, h, zz):
        return part[i, 3, zz, :, lanes(h)] + r2[i, h, 0, zz].astype(F32) + r2[i, h, 1, zz].astype(F32)

    def rs3(i, h):
        for side in range(2):
            arrived(r2.at[i, h, side], v2.at[i, h, side], s2.at[i, h, side])
        st3[i, h] = column_sum(i, h, zo).astype(BF16)
        send(st3.at[i, h], r3.at[i, h], s3.at[i, h], v3.at[i, h], across)

    def summed(i, h):
        arrived(r3.at[i, h], v3.at[i, h], s3.at[i, h])
        return hid[i, :, lanes(h)].astype(F32) + column_sum(i, h, z) + r3[i, h].astype(F32)

    def zero_terms(c, scale, h):
        product = jnp.dot(both_planes(zt, columns[c]), co[:, lanes(h)], preferred_element_type=F32)
        return (product * scale).reshape(2, WIDTH, LANES)

    normed(0, "h0")
    pl.semaphore_wait(barrier, 4)
    ag_own(0)
    normed(1, "h1")
    ag_own(1)
    normed(2, "h2")
    for k in range(2):
        w2[k, TAPS * WIDTH : KPAD, :] = jnp.zeros((KPAD - TAPS * WIDTH, C), BF16)
    shifts[TAPS * WIDTH : KPAD, :] = jnp.zeros((KPAD - TAPS * WIDTH, PIX), BF16)
    zw[WIDTH:ZPAD, :] = jnp.zeros((ZPAD - WIDTH, C), BF16)
    co[WIDTH:ZPAD, :] = jnp.zeros((ZPAD - WIDTH, PIX), BF16)
    ag_a(0)
    ag_b(0)
    ag_own(2)
    embed(0, "ctf", "cts", "cpr")
    ag_c(0)
    ag_a(1)
    ag_b(1)
    loads["cc2"].wait()
    turned(w2.at[0], w2t.at[0])
    ag_done(0)
    loads["cc1"].wait()
    conv_first(0, 0, 0)
    ag_c(1)
    conv_first(0, 0, 1)
    ag_a(2)
    ag_b(2)
    conv_first(0, 0, 2)
    second_operand(0, 1 - branch)
    conv_second(0, 0, 0)
    for h in range(PARTS):
        rs1(0, h)
    ag_c(2)
    conv_second(0, 0, 1)
    conv_second(0, 0, 2)
    for h in range(PARTS):
        rs2(0, h)
    conv_second(0, 0, 3)
    ag_done(1)
    conv_first(1, 0, 0)
    conv_first(1, 0, 1)
    for h in range(PARTS):
        rs3(0, h)
    conv_first(1, 0, 2)
    second_operand(0, branch)
    conv_second(1, 0, 0)
    for h in range(PARTS):
        rs1(1, h)
    conv_second(1, 0, 1)
    conv_second(1, 0, 2)
    for h in range(PARTS):
        rs2(1, h)
    conv_second(1, 0, 3)
    loads["zc"].wait()
    turned(zw, zt)
    scale = sc_ref[1 - branch, 0].astype(F32) * 0.125
    for h in range(PARTS):
        co[0:WIDTH, lanes(h)] = summed(0, h).astype(BF16)
    for c in range(4):
        for h in range(PARTS):
            zs[c, :, :, lanes(h)] = zero_terms(c, scale, h).astype(BF16)
    send(zs, zr, swap_send, swap_recv, partner)
    for h in range(PARTS):
        rs3(1, h)
    embed(1, "utf", "uts", "upr")
    loads["uc2"].wait()
    turned(w2.at[1], w2t.at[1])
    loads["uc1"].wait()
    ag_done(2)
    for dy in range(3):
        conv_first(2, 1, dy)
    second_operand(1, branch)
    for c in range(4):
        conv_second(2, 1, c)
    arrived(zr, swap_recv, swap_send)
    for c in range(4):
        part[2, c] += zr[c].astype(F32)
    scale = sc_ref[branch, 0].astype(F32) * 0.125
    for h in range(PARTS):
        co[0:WIDTH, lanes(h)] = summed(1, h).astype(BF16)
        part[2, 0, :, :, lanes(h)] += zero_terms(0, scale, h)
        rs1(2, h)
        for c in range(1, 4):
            part[2, c, :, :, lanes(h)] += zero_terms(c, scale, h)
    for h in range(PARTS):
        rs2(2, h)
    for h in range(PARTS):
        rs3(2, h)
    for h in range(PARTS):
        out_ref[:, lanes(h)] = summed(2, h).astype(BF16)
    for copy in sent:
        copy.wait_send()


def shards(
    unet_hidden, control_hidden, timesteps, control_scales,
    unet_time_first, unet_time_second, unet_proj, unet_conv_first, unet_conv_second,
    control_time_first, control_time_second, control_proj, control_conv_first, control_conv_second,
    zero_conv,
):
    smem = pl.BlockSpec(memory_space=pltpu.SMEM)
    hbm = pl.BlockSpec(memory_space=pl.ANY)
    dma = pltpu.SemaphoreType.DMA
    out = pl.pallas_call(
        kernel,
        out_shape=jax.ShapeDtypeStruct((WIDTH, PIX), BF16),
        in_specs=[smem, smem] + [hbm] * 13,
        out_specs=pl.BlockSpec(memory_space=pltpu.VMEM),
        scratch_shapes=[
            pltpu.VMEM((3, WIDTH, PIX), BF16),
            pltpu.VMEM((3, C, PIX), BF16),
            pltpu.VMEM((2, TAPS * WIDTH, C), BF16),
            pltpu.VMEM((2, KPAD, C), BF16),
            pltpu.VMEM((2, C, KPAD), BF16),
            pltpu.VMEM((2, TDIM, C), BF16),
            pltpu.VMEM((2, C, C), BF16),
            pltpu.VMEM((2, C, WIDTH), BF16),
            pltpu.VMEM((ZPAD, C), BF16),
            pltpu.VMEM((C, ZPAD), BF16),
            pltpu.VMEM((2, ZPAD, 128), F32),
            pltpu.VMEM((WIDTH, PIX), F32),
            pltpu.VMEM((KPAD, PIX), BF16),
            pltpu.VMEM((3, 4, 2, WIDTH, PIX), F32),
            pltpu.VMEM((ZPAD, PIX), BF16),
            pltpu.VMEM((4, 2, WIDTH, PIX), BF16),
            pltpu.VMEM((4, 2, WIDTH, PIX), BF16),
            pltpu.VMEM((3, PARTS, 2, WIDTH, LANES), BF16),
            pltpu.VMEM((3, PARTS, 2, 2, WIDTH, LANES), BF16),
            pltpu.VMEM((3, PARTS, WIDTH, LANES), BF16),
            pltpu.VMEM((3, PARTS, 2, 2, HALF, LANES), BF16),
            pltpu.VMEM((3, PARTS, 2, 2, WIDTH, LANES), BF16),
            pltpu.VMEM((3, PARTS, WIDTH, LANES), BF16),
            dma((14,)),
            dma((3, 9)),
            dma((3, 9)),
            dma((3, PARTS, 2)),
            dma((3, PARTS, 2)),
            dma((3, PARTS)),
            dma((3, PARTS, 2)),
            dma((3, PARTS, 2)),
            dma((3, PARTS)),
            dma,
            dma,
        ],
        compiler_params=pltpu.CompilerParams(
            collective_id=0, has_side_effects=True, vmem_limit_bytes=67043328
        ),
    )(
        timesteps,
        control_scales[0],
        unet_hidden[0],
        control_hidden[0].reshape(2, WIDTH, PIX),
        unet_time_first,
        unet_time_second,
        unet_proj,
        unet_conv_first.reshape(TAPS * WIDTH, C),
        unet_conv_second.reshape(TAPS * WIDTH, C),
        control_time_first[0],
        control_time_second[0],
        control_proj[0],
        control_conv_first[0].reshape(TAPS * WIDTH, C),
        control_conv_second[0].reshape(TAPS * WIDTH, C),
        zero_conv[0],
    )
    return out[None]


def solution(mesh):
    in_specs = (
        P(("branch", "dp"), "mp", None),
        P("branch", None, "dp", "mp", None),
        P(None, "dp"),
        P("branch", None, "dp"),
        P(),
        P(),
        P(None, "mp"),
        P(None, "mp", None),
        P(None, "mp", None),
        P("branch", None, None),
        P("branch", None, None),
        P("branch", None, "mp"),
        P("branch", None, "mp", None),
        P("branch", None, "mp", None),
        P("branch", "mp", None),
    )
    out_specs = P(("branch", "dp"), "mp", None)
    return jax.shard_map(shards, mesh=mesh, in_specs=in_specs, out_specs=out_specs, check_vma=False)
```

time: 138 us -> 68.4 us (0.50)
  Pallas kernels: 0 us -> 59 us
  matrix products: 37.3 us -> 0 us
  waiting for transfers between devices: 36.9 us -> 0 us
  starting transfers between devices: 26.4 us -> 0 us
  local copies, waits for them, and re-layouts: 22.6 us -> 8.3 us
  other arithmetic: 12 us -> 0 us
    pallas_call x0 -> x1, Pallas kernels: none -> 59 us  [shards(): pl.pallas_call(kernel, out_shape=jax.ShapeDtypeStruct((WIDTH, PIX), BF16)...]
    dot_general x42 -> x0, matrix products: 37.3 us -> none  [the longest x36 28.5 us: conv_taps(): jnp.einsum(einsum_form, weight[tap_index], window, preferred_element_type...]
    all_to_all x5 -> x0, waiting for transfers between devices: 36.9 us -> none  [the longest x3 36.9 us: sent_and_summed(): pieces = lax.all_to_all(split_up(array, dim, peers), axis, 0, 0, tiled=True)]
    all_to_all x5 -> x0, starting transfers between devices: 26.4 us -> none  [the longest x3 14.7 us: sent_and_summed(): pieces = lax.all_to_all(split_up(array, dim, peers), axis, 0, 0, tiled=True)]
    reduce_sum x17 -> x0, other arithmetic: 6.81 us -> none  [the longest x3 2.87 us: sent_and_summed(): return jnp.sum(pieces.astype(jnp.float32), axis=0)]
    unnamed x32 -> x4, local copies, waits for them, and re-layouts: 1.06 us -> 6.99 us
    slice x4 -> x0, local copies, waits for them, and re-layouts: 5.82 us -> none  [conv_taps(): padded[:, :, row_shift:row_shift + SIDE, col_shift:col_shift + SIDE]]
    transpose x3 -> x0, local copies, waits for them, and re-layouts: 4.16 us -> none  [the longest x2 3.01 us: joined_along(): pieces = jnp.moveaxis(pieces, 0, dim)]
  transfers between devices with their start and end apart: 5 -> 0, of which waited for: 3 -> 0; matrix products, arithmetic and copies ran while one was open for 29% -> 0% of each run, Pallas kernels for 0% -> 0%
where the time goes in v1:
time: 68.4 us; the launch traced here: 67.3 us
  Pallas kernels  59 us (86%)
  local copies, waits for them, and re-layouts  8.3 us (12%)
    pallas_call x1, Pallas kernels, shards(): pl.pallas_call(kernel, out_shape=jax.ShapeDtypeStruct((WIDTH, PIX), BF16)...  59 us
    unnamed x4, local copies, waits for them, and re-layouts  6.99 us

profile of v1, /device:TPU:0, one launch (start us, length us, event | category | flops | bytes accessed | tf_op | source)
XLA Modules:
  0.0 67.3 jit_solution(16076374435706395251)
XLA Ops:
  0.0 1.3 %copy.17.ts_ref = s32[2,1]{1,0:T(2,128)} copy(s32[2,1]{0,1:T(1,128)} %param.17) | data formatting | bytes 16 | tf_op args[2]
  1.3 1.3 %copy.18.sc_ref = s32[2,1]{1,0:T(2,128)} copy(s32[2,1]{0,1:T(1,128)} %bitcast.23) | data formatting | bytes 16 | tf_op jit(solution)/shard_map/squeeze | solution.py:399
  2.6 2.1 %copy.19.upr = bf16[1280,160]{1,0:T(8,128)(2,1)} copy(bf16[1280,160]{0,1:T(8,128)(2,1)} %param.21) | data formatting | bytes 819200 | tf_op args[6]
  4.7 2.1 %copy.16 = bf16[1,1280,160]{2,1,0:T(8,128)(2,1)} copy(bf16[1,1280,160]{1,2,0:T(8,128)(2,1)} %param.26) | data formatting | bytes 819200 | tf_op args[11]
  6.8 59.0 %shard_map.145 = bf16[160,256]{1,0:T(8,128)(2,1)} custom-call(s32[2,1]{1,0:T(2,128)} %copy.17.ts_ref, s32[2,1]{1,0:T(2,128)} %copy.18.sc_ref, bf16[160,256]{1,0:T(8,128)(2,1)} %bitcast.22, bf16[2,160,256]{2,1,0:T(8,128)(2,1)} %bitcast.21, bf16[320,1280]{1,0:T(8,128)(2,1)} %utf.1, bf16[1280,1280]{1,0:T(8,128)(2,1)} %uts.1, bf16[1280,160]{1,0:T(8,128)(2,1)} %copy.19.upr, ...), custom_call_target="tpu_custom_call" | custom-call | tf_op jit(solution)/shard_map/pallas_call | solution.py:353
  65.8 1.5 %copy.21 = bf16[1,160,256]{2,1,0:T(8,128)(2,1)} copy(bf16[1,160,256]{2,1,0:T(8,128)(2,1)} %bitcast.20) | data formatting | bytes 163840

commit v2 on v1

--- a/solution.py
+++ b/solution.py
@@ -58,6 +58,8 @@
     up = {"mp": z * 4 + yp}
     down = {"mp": z * 4 + ym}
     across = {"mp": zo * 4 + y}
+    across_up = {"mp": zo * 4 + yp}
+    across_down = {"mp": zo * 4 + ym}
     partner = {"branch": 1 - branch}
     columns = (y2, yp, ym, y)
 
@@ -122,24 +124,25 @@
         send(got, got, ag_send.at[i, 3], ag_recv.at[i, 3], up)
         send(got, got, ag_send.at[i, 4], ag_recv.at[i, 4], down)
 
-    def ag_relay(i, zz, first, second):
-        arrived(piece(i, zz, ym), ag_recv.at[i, first], ag_send.at[i, first])
-        low = piece(i, zz, ym, 0, HALF)
-        send(low, low, ag_send.at[i, second], ag_recv.at[i, second], up)
-        arrived(piece(i, zz, yp), ag_recv.at[i, first + 1], ag_send.at[i, first + 1])
-        high = piece(i, zz, yp, HALF, HALF)
-        send(high, high, ag_send.at[i, second + 1], ag_recv.at[i, second + 1], down)
-
     def ag_b(i):
-        ag_relay(i, z, 1, 5)
+        arrived(piece(i, z, ym), ag_recv.at[i, 1], ag_send.at[i, 1])
+        low = piece(i, z, ym, 0, HALF)
+        send(low, low, ag_send.at[i, 5], ag_recv.at[i, 5], up)
+        arrived(piece(i, z, yp), ag_recv.at[i, 2], ag_send.at[i, 2])
+        high = piece(i, z, yp, HALF, HALF)
+        send(high, high, ag_send.at[i, 6], ag_recv.at[i, 6], down)
 
     def ag_c(i):
-        ag_relay(i, zo, 3, 7)
+        for k in range(2):
+            got = piece(i, z, y2, k * HALF, HALF)
+            arrived(got, ag_recv.at[i, 5 + k], ag_send.at[i, 5 + k])
+            send(got, got, ag_send.at[i, 7 + k], ag_recv.at[i, 7 + k], across)
 
     def ag_done(i):
-        for zz, first in ((z, 5), (zo, 7)):
-            arrived(piece(i, zz, y2, 0, HALF), ag_recv.at[i, first], ag_send.at[i, first])
-            arrived(piece(i, zz, y2, HALF, HALF), ag_recv.at[i, first + 1], ag_send.at[i, first + 1])
+        arrived(piece(i, zo, ym), ag_recv.at[i, 3], ag_send.at[i, 3])
+        arrived(piece(i, zo, yp), ag_recv.at[i, 4], ag_send.at[i, 4])
+        for k in range(2):
+            arrived(piece(i, zo, y2, k * HALF, HALF), ag_recv.at[i, 7 + k], ag_send.at[i, 7 + k])
 
     pixel = lax.broadcasted_iota(jnp.int32, (1, PIX), 1)
     column = pixel % SIDE
@@ -152,7 +155,7 @@
         half_width = TDIM // 2
         index = jnp.where(lane < half_width, lane, lane - half_width).astype(F32)
         frequency = jnp.exp(-math.log(10000.0) * index / half_width)
-        step = jnp.where(row == 0, ts_ref[0, 0].astype(F32), ts_ref[1, 0].astype(F32))
+        step = jnp.where(row == 0, ts_ref[0, 0].astype(F32), ts_ref[0, 1].astype(F32))
         angle = step * frequency
         return jnp.where(lane < half_width, jnp.cos(angle), jnp.sin(angle)).astype(BF16)
 
@@ -162,14 +165,11 @@
         loads[second].wait()
         time_act = silu(jnp.dot(middle, tw[k], preferred_element_type=F32)).astype(BF16)
         loads[third].wait()
-        projected = jnp.dot(time_act, pr[k], preferred_element_type=F32)
-        wide = jnp.concatenate([projected, jnp.zeros((16, ZPAD - WIDTH), F32)], axis=1)
-        tall = jnp.concatenate([wide, jnp.zeros((128 - 16, ZPAD), F32)], axis=0)
-        tpt[k] = tall.T
+        tpt[k] = lax.dot_general(pr[k], time_act, (((1,), (1,)), ((), ())), preferred_element_type=F32)
 
     def time_column(k, half):
-        lane = lax.broadcasted_iota(jnp.int32, (WIDTH, 128), 1)
-        return jnp.sum(jnp.where(lane == half, tpt[k, 0:WIDTH, :], 0.0), axis=1, keepdims=True)
+        lane = lax.broadcasted_iota(jnp.int32, (WIDTH, 16), 1)
+        return jnp.sum(jnp.where(lane == half, tpt[k], 0.0), axis=1, keepdims=True)
 
     def turned(src, dst):
         def body(j, carry):
@@ -219,8 +219,12 @@
         send(st1.at[i, h, :, pl.ds(0, HALF)], r1.at[i, h, 0], s1.at[i, h, 0], v1.at[i, h, 0], up)
         send(st1.at[i, h, :, pl.ds(HALF, HALF)], r1.at[i, h, 1], s1.at[i, h, 1], v1.at[i, h, 1], down)
 
+    def rsz(i, h):
+        st3[i, h] = part[i, 3, zo, :, lanes(h)].astype(BF16)
+        send(st3.at[i, h], r3.at[i, h], s3.at[i, h], v3.at[i, h], across)
+
     def rs2(i, h):
-        for side, target in ((0, up), (1, down)):
+        for side, near, far in ((0, up, across_up), (1, down, across_down)):
             arrived(r1.at[i, h, side], v1.at[i, h, side], s1.at[i, h, side])
             plus = slice(side * HALF, (side + 1) * HALF)
             other = slice((1 - side) * HALF, (2 - side) * HALF)
@@ -228,20 +232,21 @@
                 part[i, 1 + side, :, plus, lanes(h)] + r1[i, h, side].astype(F32)
             ).astype(BF16)
             st2[i, h, side, :, other, :] = part[i, 1 + side, :, other, lanes(h)].astype(BF16)
-            send(st2.at[i, h, side], r2.at[i, h, side], s2.at[i, h, side], v2.at[i, h, side], target)
-
-    def column_sum(i, h, zz):
-        return part[i, 3, zz, :, lanes(h)] + r2[i, h, 0, zz].astype(F32) + r2[i, h, 1, zz].astype(F32)
-
-    def rs3(i, h):
-        for side in range(2):
-            arrived(r2.at[i, h, side], v2.at[i, h, side], s2.at[i, h, side])
-        st3[i, h] = column_sum(i, h, zo).astype(BF16)
-        send(st3.at[i, h], r3.at[i, h], s3.at[i, h], v3.at[i, h], across)
+            for plane, zz, target in ((1, zo, far), (0, z, near)):
+                send(
+                    st2.at[i, h, side, zz], r2.at[i, h, side, plane],
+                    s2.at[i, h, side, plane], v2.at[i, h, side, plane], target,
+                )
 
     def summed(i, h):
+        total = hid[i, :, lanes(h)].astype(F32) + part[i, 3, z, :, lanes(h)]
         arrived(r3.at[i, h], v3.at[i, h], s3.at[i, h])
-        return hid[i, :, lanes(h)].astype(F32) + column_sum(i, h, z) + r3[i, h].astype(F32)
+        total = total + r3[i, h].astype(F32)
+        for plane in range(2):
+            for side in range(2):
+                arrived(r2.at[i, h, side, plane], v2.at[i, h, side, plane], s2.at[i, h, side, plane])
+                total = total + r2[i, h, side, plane].astype(F32)
+        return total
 
     def zero_terms(c, scale, h):
         product = jnp.dot(both_planes(zt, columns[c]), co[:, lanes(h)], preferred_element_type=F32)
@@ -260,57 +265,57 @@
     co[WIDTH:ZPAD, :] = jnp.zeros((ZPAD - WIDTH, PIX), BF16)
     ag_a(0)
     ag_b(0)
-    ag_own(2)
     embed(0, "ctf", "cts", "cpr")
     ag_c(0)
     ag_a(1)
     ag_b(1)
+    ag_own(2)
     loads["cc2"].wait()
     turned(w2.at[0], w2t.at[0])
+    loads["cc1"].wait()
+    ag_c(1)
     ag_done(0)
-    loads["cc1"].wait()
     conv_first(0, 0, 0)
-    ag_c(1)
     conv_first(0, 0, 1)
     ag_a(2)
+    conv_first(0, 0, 2)
     ag_b(2)
-    conv_first(0, 0, 2)
     second_operand(0, 1 - branch)
     conv_second(0, 0, 0)
     for h in range(PARTS):
         rs1(0, h)
-    ag_c(2)
+    conv_second(0, 0, 3)
+    for h in range(PARTS):
+        rsz(0, h)
     conv_second(0, 0, 1)
     conv_second(0, 0, 2)
-    for h in range(PARTS):
-        rs2(0, h)
-    conv_second(0, 0, 3)
+    ag_c(2)
     ag_done(1)
     conv_first(1, 0, 0)
+    for h in range(PARTS):
+        rs2(0, h)
     conv_first(1, 0, 1)
-    for h in range(PARTS):
-        rs3(0, h)
     conv_first(1, 0, 2)
     second_operand(0, branch)
     conv_second(1, 0, 0)
     for h in range(PARTS):
         rs1(1, h)
+    conv_second(1, 0, 3)
+    for h in range(PARTS):
+        rsz(1, h)
     conv_second(1, 0, 1)
     conv_second(1, 0, 2)
-    for h in range(PARTS):
-        rs2(1, h)
-    conv_second(1, 0, 3)
     loads["zc"].wait()
     turned(zw, zt)
-    scale = sc_ref[1 - branch, 0].astype(F32) * 0.125
+    for h in range(PARTS):
+        rs2(1, h)
+    scale = sc_ref[0, 1 - branch].astype(F32) * 0.125
     for h in range(PARTS):
         co[0:WIDTH, lanes(h)] = summed(0, h).astype(BF16)
     for c in range(4):
         for h in range(PARTS):
             zs[c, :, :, lanes(h)] = zero_terms(c, scale, h).astype(BF16)
     send(zs, zr, swap_send, swap_recv, partner)
-    for h in range(PARTS):
-        rs3(1, h)
     embed(1, "utf", "uts", "upr")
     loads["uc2"].wait()
     turned(w2.at[1], w2t.at[1])
@@ -324,17 +329,17 @@
     arrived(zr, swap_recv, swap_send)
     for c in range(4):
         part[2, c] += zr[c].astype(F32)
-    scale = sc_ref[branch, 0].astype(F32) * 0.125
+    scale = sc_ref[0, branch].astype(F32) * 0.125
     for h in range(PARTS):
         co[0:WIDTH, lanes(h)] = summed(1, h).astype(BF16)
         part[2, 0, :, :, lanes(h)] += zero_terms(0, scale, h)
         rs1(2, h)
-        for c in range(1, 4):
+        part[2, 3, :, :, lanes(h)] += zero_terms(3, scale, h)
+        rsz(2, h)
+        for c in range(1, 3):
             part[2, c, :, :, lanes(h)] += zero_terms(c, scale, h)
     for h in range(PARTS):
         rs2(2, h)
-    for h in range(PARTS):
-        rs3(2, h)
     for h in range(PARTS):
         out_ref[:, lanes(h)] = summed(2, h).astype(BF16)
     for copy in sent:
@@ -363,10 +368,10 @@
             pltpu.VMEM((2, C, KPAD), BF16),
             pltpu.VMEM((2, TDIM, C), BF16),
             pltpu.VMEM((2, C, C), BF16),
-            pltpu.VMEM((2, C, WIDTH), BF16),
+            pltpu.VMEM((2, WIDTH, C), BF16),
             pltpu.VMEM((ZPAD, C), BF16),
             pltpu.VMEM((C, ZPAD), BF16),
-            pltpu.VMEM((2, ZPAD, 128), F32),
+            pltpu.VMEM((2, WIDTH, 16), F32),
             pltpu.VMEM((WIDTH, PIX), F32),
             pltpu.VMEM((KPAD, PIX), BF16),
             pltpu.VMEM((3, 4, 2, WIDTH, PIX), F32),
@@ -383,10 +388,10 @@
             dma((3, 9)),
             dma((3, 9)),
             dma((3, PARTS, 2)),
-            dma((3, PARTS, 2)),
+            dma((3, PARTS, 2, 2)),
             dma((3, PARTS)),
             dma((3, PARTS, 2)),
-            dma((3, PARTS, 2)),
+            dma((3, PARTS, 2, 2)),
             dma((3, PARTS)),
             dma,
             dma,
@@ -395,18 +400,18 @@
             collective_id=0, has_side_effects=True, vmem_limit_bytes=67043328
         ),
     )(
-        timesteps,
-        control_scales[0],
+        timesteps.reshape(1, 2),
+        control_scales.reshape(1, 2),
         unet_hidden[0],
         control_hidden[0].reshape(2, WIDTH, PIX),
         unet_time_first,
         unet_time_second,
-        unet_proj,
+        unet_proj.T,
         unet_conv_first.reshape(TAPS * WIDTH, C),
         unet_conv_second.reshape(TAPS * WIDTH, C),
         control_time_first[0],
         control_time_second[0],
-        control_proj[0],
+        control_proj[0].T,
         control_conv_first[0].reshape(TAPS * WIDTH, C),
         control_conv_second[0].reshape(TAPS * WIDTH, C),
         zero_conv[0],

time: 68.4 us -> 51.2 us (0.75); the launches traced: 67.3 us -> 51.1 us
  Pallas kernels: 59 us -> 49.6 us
  local copies, waits for them, and re-layouts: 8.3 us -> 1.53 us
    pallas_call x1, Pallas kernels: 59 us -> 49.6 us  [shards(): pl.pallas_call(kernel, out_shape=jax.ShapeDtypeStruct((WIDTH, PIX), BF16)...]
    unnamed x4 -> x1, local copies, waits for them, and re-layouts: 6.99 us -> 1.53 us
    squeeze x1 -> x0, local copies, waits for them, and re-layouts: 1.31 us -> none  [shards(): control_scales[0]]
where the time goes in v2:
time: 51.2 us; the launch traced here: 51.1 us
  Pallas kernels  49.6 us (97%)
  local copies, waits for them, and re-layouts  1.53 us (3%)
    pallas_call x1, Pallas kernels, shards(): pl.pallas_call(kernel, out_shape=jax.ShapeDtypeStruct((WIDTH, PIX), BF16)...  49.6 us
    unnamed x1, local copies, waits for them, and re-layouts  1.53 us

profile of v2, /device:TPU:0, one launch (start us, length us, event | category | flops | bytes accessed | tf_op | source)
XLA Modules:
  0.0 51.1 jit_solution(8839266378403301528)
XLA Ops:
  0.0 49.6 %shard_map.145 = bf16[160,256]{1,0:T(8,128)(2,1)} custom-call(s32[1,2]{1,0:T(1,128)} %bitcast.28, s32[1,2]{1,0:T(1,128)} %bitcast.29, bf16[160,256]{1,0:T(8,128)(2,1)} %bitcast.27, bf16[2,160,256]{2,1,0:T(8,128)(2,1)} %bitcast.26, bf16[320,1280]{1,0:T(8,128)(2,1)} %utf.1, bf16[1280,1280]{1,0:T(8,128)(2,1)} %uts.1, bf16[160,1280]{1,0:T(8,128)(2,1)} %bitcast.22, ...), custom_call_target="tpu_custom_call" | custom-call | tf_op jit(solution)/shard_map/pallas_call | solution.py:358
  49.6 1.5 %copy.17 = bf16[1,160,256]{2,1,0:T(8,128)(2,1)} copy(bf16[1,160,256]{2,1,0:T(8,128)(2,1)} %bitcast.25) | data formatting | bytes 163840

commit v3 on v2

--- a/solution.py
+++ b/solution.py
@@ -47,7 +47,7 @@
     out_ref,
     hid, act, w1, w2, w2t, tf, tw, pr, zw, zt, tpt, inner, shifts, part, co, zs, zr,
     st1, st2, st3, r1, r2, r3,
-    load_sem, ag_send, ag_recv, s1, s2, s3, v1, v2, v3, swap_send, swap_recv,
+    gate, load_sem, ag_send, ag_recv, s1, s2, s3, v1, v2, v3, swap_send, swap_recv,
 ):
     branch = lax.axis_index("branch")
     spot = lax.axis_index("mp")
@@ -112,37 +112,29 @@
         loads[name].wait()
         act[i, pl.ds(rows(z, y), WIDTH), :] = norm_silu(hid[i].astype(F32)).astype(BF16)
 
-    def ag_own(i):
+    def ag_near(i):
         own = piece(i, z, y)
-        send(own, own, ag_send.at[i, 0], ag_recv.at[i, 0], across)
-        send(own, own, ag_send.at[i, 1], ag_recv.at[i, 1], up)
-        send(own, own, ag_send.at[i, 2], ag_recv.at[i, 2], down)
-
-    def ag_a(i):
-        got = piece(i, zo, y)
-        arrived(got, ag_recv.at[i, 0], ag_send.at[i, 0])
-        send(got, got, ag_send.at[i, 3], ag_recv.at[i, 3], up)
-        send(got, got, ag_send.at[i, 4], ag_recv.at[i, 4], down)
-
-    def ag_b(i):
-        arrived(piece(i, z, ym), ag_recv.at[i, 1], ag_send.at[i, 1])
-        low = piece(i, z, ym, 0, HALF)
-        send(low, low, ag_send.at[i, 5], ag_recv.at[i, 5], up)
-        arrived(piece(i, z, yp), ag_recv.at[i, 2], ag_send.at[i, 2])
-        high = piece(i, z, yp, HALF, HALF)
-        send(high, high, ag_send.at[i, 6], ag_recv.at[i, 6], down)
-
-    def ag_c(i):
-        for k in range(2):
-            got = piece(i, z, y2, k * HALF, HALF)
-            arrived(got, ag_recv.at[i, 5 + k], ag_send.at[i, 5 + k])
-            send(got, got, ag_send.at[i, 7 + k], ag_recv.at[i, 7 + k], across)
+        for k, target in ((1, up), (2, down), (0, across)):
+            send(own, own, ag_send.at[i, k], ag_recv.at[i, k], target)
+
+    def ag_far(i):
+        own = piece(i, z, y)
+        for k, target in ((3, across_up), (4, across_down)):
+            send(own, own, ag_send.at[i, k], ag_recv.at[i, k], target)
+
+    def ag_relay(i, k):
+        zz = z if k < 3 else zo
+        side = (k - 1) % 2
+        source, target = ((ym, up), (yp, down))[side]
+        arrived(piece(i, zz, source), ag_recv.at[i, k], ag_send.at[i, k])
+        half = piece(i, zz, source, side * HALF, HALF)
+        send(half, half, ag_send.at[i, k + 4], ag_recv.at[i, k + 4], target)
 
     def ag_done(i):
-        arrived(piece(i, zo, ym), ag_recv.at[i, 3], ag_send.at[i, 3])
-        arrived(piece(i, zo, yp), ag_recv.at[i, 4], ag_send.at[i, 4])
-        for k in range(2):
-            arrived(piece(i, zo, y2, k * HALF, HALF), ag_recv.at[i, 7 + k], ag_send.at[i, 7 + k])
+        arrived(piece(i, zo, y), ag_recv.at[i, 0], ag_send.at[i, 0])
+        for zz, first in ((z, 5), (zo, 7)):
+            for k in range(2):
+                arrived(piece(i, zz, y2, k * HALF, HALF), ag_recv.at[i, first + k], ag_send.at[i, first + k])
 
     pixel = lax.broadcasted_iota(jnp.int32, (1, PIX), 1)
     column = pixel % SIDE
@@ -223,20 +215,20 @@
         st3[i, h] = part[i, 3, zo, :, lanes(h)].astype(BF16)
         send(st3.at[i, h], r3.at[i, h], s3.at[i, h], v3.at[i, h], across)
 
-    def rs2(i, h):
-        for side, near, far in ((0, up, across_up), (1, down, across_down)):
-            arrived(r1.at[i, h, side], v1.at[i, h, side], s1.at[i, h, side])
-            plus = slice(side * HALF, (side + 1) * HALF)
-            other = slice((1 - side) * HALF, (2 - side) * HALF)
-            st2[i, h, side, :, plus, :] = (
-                part[i, 1 + side, :, plus, lanes(h)] + r1[i, h, side].astype(F32)
-            ).astype(BF16)
-            st2[i, h, side, :, other, :] = part[i, 1 + side, :, other, lanes(h)].astype(BF16)
-            for plane, zz, target in ((1, zo, far), (0, z, near)):
-                send(
-                    st2.at[i, h, side, zz], r2.at[i, h, side, plane],
-                    s2.at[i, h, side, plane], v2.at[i, h, side, plane], target,
-                )
+    def rs2(i, h, side):
+        near, far = ((up, across_up), (down, across_down))[side]
+        arrived(r1.at[i, h, side], v1.at[i, h, side], s1.at[i, h, side])
+        plus = slice(side * HALF, (side + 1) * HALF)
+        other = slice((1 - side) * HALF, (2 - side) * HALF)
+        st2[i, h, side, :, plus, :] = (
+            part[i, 1 + side, :, plus, lanes(h)] + r1[i, h, side].astype(F32)
+        ).astype(BF16)
+        st2[i, h, side, :, other, :] = part[i, 1 + side, :, other, lanes(h)].astype(BF16)
+        for plane, zz, target in ((1, zo, far), (0, z, near)):
+            send(
+                st2.at[i, h, side, zz], r2.at[i, h, side, plane],
+                s2.at[i, h, side, plane], v2.at[i, h, side, plane], target,
+            )
 
     def summed(i, h):
         total = hid[i, :, lanes(h)].astype(F32) + part[i, 3, z, :, lanes(h)]
@@ -248,100 +240,156 @@
                 total = total + r2[i, h, side, plane].astype(F32)
         return total
 
-    def zero_terms(c, scale, h):
-        product = jnp.dot(both_planes(zt, columns[c]), co[:, lanes(h)], preferred_element_type=F32)
+    def zero_terms(i, c, h):
+        scale = sc_ref[0, 1 - branch if i == 0 else branch].astype(F32) * 0.125
+        product = jnp.dot(both_planes(zt, columns[c]), co[i, :, lanes(h)], preferred_element_type=F32)
         return (product * scale).reshape(2, WIDTH, LANES)
+
+    def copy_out(i, h):
+        co[i, 0:WIDTH, lanes(h)] = summed(i, h).astype(BF16)
+
+    def swap(h):
+        copy_out(0, h)
+        for c in range(4):
+            zs[h, c] = zero_terms(0, c, h).astype(BF16)
+        send(zs.at[h], zr.at[h], swap_send.at[h], swap_recv.at[h], partner)
+
+    def swapped(h):
+        arrived(zr.at[h], swap_recv.at[h], swap_send.at[h])
+        for c in range(4):
+            part[2, c, :, :, lanes(h)] += zr[h, c].astype(F32)
+
+    def with_zero(c, h):
+        part[2, c, :, :, lanes(h)] += zero_terms(1, c, h)
 
     normed(0, "h0")
     pl.semaphore_wait(barrier, 4)
-    ag_own(0)
+    ag_near(0)
+    pl.semaphore_signal(gate, inc=1, device_id=across, device_id_type=MESH)
     normed(1, "h1")
-    ag_own(1)
     normed(2, "h2")
+    pl.semaphore_wait(gate, 1)
+    ag_far(0)
+    ag_near(1)
+    ag_far(1)
     for k in range(2):
         w2[k, TAPS * WIDTH : KPAD, :] = jnp.zeros((KPAD - TAPS * WIDTH, C), BF16)
+        co[k, WIDTH:ZPAD, :] = jnp.zeros((ZPAD - WIDTH, PIX), BF16)
     shifts[TAPS * WIDTH : KPAD, :] = jnp.zeros((KPAD - TAPS * WIDTH, PIX), BF16)
     zw[WIDTH:ZPAD, :] = jnp.zeros((ZPAD - WIDTH, C), BF16)
-    co[WIDTH:ZPAD, :] = jnp.zeros((ZPAD - WIDTH, PIX), BF16)
-    ag_a(0)
-    ag_b(0)
     embed(0, "ctf", "cts", "cpr")
-    ag_c(0)
-    ag_a(1)
-    ag_b(1)
-    ag_own(2)
+    ag_relay(0, 1)
+    ag_relay(0, 2)
+    ag_relay(0, 3)
+    ag_relay(0, 4)
     loads["cc2"].wait()
     turned(w2.at[0], w2t.at[0])
     loads["cc1"].wait()
-    ag_c(1)
+    ag_relay(1, 1)
+    ag_relay(1, 2)
+    ag_near(2)
+    ag_far(2)
     ag_done(0)
-    conv_first(0, 0, 0)
-    conv_first(0, 0, 1)
-    ag_a(2)
-    conv_first(0, 0, 2)
-    ag_b(2)
-    second_operand(0, 1 - branch)
-    conv_second(0, 0, 0)
-    for h in range(PARTS):
-        rs1(0, h)
-    conv_second(0, 0, 3)
-    for h in range(PARTS):
-        rsz(0, h)
-    conv_second(0, 0, 1)
-    conv_second(0, 0, 2)
-    ag_c(2)
+    @pl.when(branch < 2)
+    def _():
+        conv_first(0, 0, 0)
+        conv_first(0, 0, 1)
+        conv_first(0, 0, 2)
+    ag_relay(1, 3)
+    ag_relay(1, 4)
+    @pl.when(branch < 2)
+    def _():
+        second_operand(0, 1 - branch)
+    @pl.when(branch < 2)
+    def _():
+        conv_second(0, 0, 0)
+        conv_second(0, 0, 3)
+    rs1(0, 0)
+    rs1(0, 1)
+    rsz(0, 0)
+    rsz(0, 1)
+    @pl.when(branch < 2)
+    def _():
+        conv_second(0, 0, 1)
+        conv_second(0, 0, 2)
+    ag_relay(2, 1)
+    ag_relay(2, 2)
     ag_done(1)
-    conv_first(1, 0, 0)
-    for h in range(PARTS):
-        rs2(0, h)
-    conv_first(1, 0, 1)
-    conv_first(1, 0, 2)
-    second_operand(0, branch)
-    conv_second(1, 0, 0)
-    for h in range(PARTS):
-        rs1(1, h)
-    conv_second(1, 0, 3)
-    for h in range(PARTS):
-        rsz(1, h)
-    conv_second(1, 0, 1)
-    conv_second(1, 0, 2)
+    @pl.when(branch < 2)
+    def _():
+        conv_first(1, 0, 0)
+        conv_first(1, 0, 1)
+        conv_first(1, 0, 2)
+    rs2(0, 0, 0)
+    rs2(0, 0, 1)
+    ag_relay(2, 3)
+    ag_relay(2, 4)
+    @pl.when(branch < 2)
+    def _():
+        second_operand(0, branch)
+    @pl.when(branch < 2)
+    def _():
+        conv_second(1, 0, 0)
+        conv_second(1, 0, 3)
+    rs1(1, 0)
+    rs1(1, 1)
+    rsz(1, 0)
+    rsz(1, 1)
+    @pl.when(branch < 2)
+    def _():
+        conv_second(1, 0, 1)
+        conv_second(1, 0, 2)
+    rs2(0, 1, 0)
+    rs2(0, 1, 1)
     loads["zc"].wait()
     turned(zw, zt)
-    for h in range(PARTS):
-        rs2(1, h)
-    scale = sc_ref[0, 1 - branch].astype(F32) * 0.125
-    for h in range(PARTS):
-        co[0:WIDTH, lanes(h)] = summed(0, h).astype(BF16)
-    for c in range(4):
-        for h in range(PARTS):
-            zs[c, :, :, lanes(h)] = zero_terms(c, scale, h).astype(BF16)
-    send(zs, zr, swap_send, swap_recv, partner)
-    embed(1, "utf", "uts", "upr")
     loads["uc2"].wait()
     turned(w2.at[1], w2t.at[1])
+    embed(1, "utf", "uts", "upr")
+    rs2(1, 0, 0)
+    rs2(1, 0, 1)
+    rs2(1, 1, 0)
+    rs2(1, 1, 1)
     loads["uc1"].wait()
     ag_done(2)
-    for dy in range(3):
-        conv_first(2, 1, dy)
-    second_operand(1, branch)
-    for c in range(4):
-        conv_second(2, 1, c)
-    arrived(zr, swap_recv, swap_send)
-    for c in range(4):
-        part[2, c] += zr[c].astype(F32)
-    scale = sc_ref[0, branch].astype(F32) * 0.125
-    for h in range(PARTS):
-        co[0:WIDTH, lanes(h)] = summed(1, h).astype(BF16)
-        part[2, 0, :, :, lanes(h)] += zero_terms(0, scale, h)
-        rs1(2, h)
-        part[2, 3, :, :, lanes(h)] += zero_terms(3, scale, h)
-        rsz(2, h)
-        for c in range(1, 3):
-            part[2, c, :, :, lanes(h)] += zero_terms(c, scale, h)
-    for h in range(PARTS):
-        rs2(2, h)
-    for h in range(PARTS):
-        out_ref[:, lanes(h)] = summed(2, h).astype(BF16)
+    @pl.when(branch < 2)
+    def _():
+        conv_first(2, 1, 0)
+        conv_first(2, 1, 1)
+        conv_first(2, 1, 2)
+    swap(0)
+    swap(1)
+    @pl.when(branch < 2)
+    def _():
+        second_operand(1, branch)
+    @pl.when(branch < 2)
+    def _():
+        conv_second(2, 1, 0)
+        conv_second(2, 1, 3)
+        conv_second(2, 1, 1)
+        conv_second(2, 1, 2)
+    swapped(0)
+    swapped(1)
+    copy_out(1, 0)
+    with_zero(0, 0)
+    rs1(2, 0)
+    with_zero(3, 0)
+    rsz(2, 0)
+    with_zero(1, 0)
+    with_zero(2, 0)
+    copy_out(1, 1)
+    with_zero(0, 1)
+    rs1(2, 1)
+    with_zero(3, 1)
+    rsz(2, 1)
+    with_zero(1, 1)
+    with_zero(2, 1)
+    rs2(2, 0, 0)
+    rs2(2, 0, 1)
+    rs2(2, 1, 0)
+    rs2(2, 1, 1)
+    out_ref[:, lanes(0)] = summed(2, 0).astype(BF16)
+    out_ref[:, lanes(1)] = summed(2, 1).astype(BF16)
     for copy in sent:
         copy.wait_send()
 
@@ -375,15 +423,16 @@
             pltpu.VMEM((WIDTH, PIX), F32),
             pltpu.VMEM((KPAD, PIX), BF16),
             pltpu.VMEM((3, 4, 2, WIDTH, PIX), F32),
-            pltpu.VMEM((ZPAD, PIX), BF16),
-            pltpu.VMEM((4, 2, WIDTH, PIX), BF16),
-            pltpu.VMEM((4, 2, WIDTH, PIX), BF16),
+            pltpu.VMEM((2, ZPAD, PIX), BF16),
+            pltpu.VMEM((PARTS, 4, 2, WIDTH, LANES), BF16),
+            pltpu.VMEM((PARTS, 4, 2, WIDTH, LANES), BF16),
             pltpu.VMEM((3, PARTS, 2, WIDTH, LANES), BF16),
             pltpu.VMEM((3, PARTS, 2, 2, WIDTH, LANES), BF16),
             pltpu.VMEM((3, PARTS, WIDTH, LANES), BF16),
             pltpu.VMEM((3, PARTS, 2, 2, HALF, LANES), BF16),
             pltpu.VMEM((3, PARTS, 2, 2, WIDTH, LANES), BF16),
             pltpu.VMEM((3, PARTS, WIDTH, LANES), BF16),
+            pltpu.SemaphoreType.REGULAR,
             dma((14,)),
             dma((3, 9)),
             dma((3, 9)),
@@ -393,8 +442,8 @@
             dma((3, PARTS, 2)),
             dma((3, PARTS, 2, 2)),
             dma((3, PARTS)),
-            dma,
-            dma,
+            dma((PARTS,)),
+            dma((PARTS,)),
         ],
         compiler_params=pltpu.CompilerParams(
             collective_id=0, has_side_effects=True, vmem_limit_bytes=67043328

time: 51.2 us -> 45.4 us (0.89)
  Pallas kernels: 49.6 us -> 43.7 us
    pallas_call x1, Pallas kernels: 49.6 us -> 43.7 us  [shards(): pl.pallas_call(kernel, out_shape=jax.ShapeDtypeStruct((WIDTH, PIX), BF16)...]
where the time goes in v3:
time: 45.4 us; the launch traced here: 45.2 us
  Pallas kernels  43.7 us (96%)
  local copies, waits for them, and re-layouts  1.53 us (3%)
    pallas_call x1, Pallas kernels, shards(): pl.pallas_call(kernel, out_shape=jax.ShapeDtypeStruct((WIDTH, PIX), BF16)...  43.7 us
    unnamed x1, local copies, waits for them, and re-layouts  1.53 us

profile of v3, /device:TPU:0, one launch (start us, length us, event | category | flops | bytes accessed | tf_op | source)
XLA Modules:
  0.0 45.2 jit_solution(7747774879516892520)
XLA Ops:
  0.0 43.7 %shard_map.145 = bf16[160,256]{1,0:T(8,128)(2,1)} custom-call(s32[1,2]{1,0:T(1,128)} %bitcast.28, s32[1,2]{1,0:T(1,128)} %bitcast.29, bf16[160,256]{1,0:T(8,128)(2,1)} %bitcast.27, bf16[2,160,256]{2,1,0:T(8,128)(2,1)} %bitcast.26, bf16[320,1280]{1,0:T(8,128)(2,1)} %utf.1, bf16[1280,1280]{1,0:T(8,128)(2,1)} %uts.1, bf16[160,1280]{1,0:T(8,128)(2,1)} %bitcast.22, ...), custom_call_target="tpu_custom_call" | custom-call | tf_op jit(solution)/shard_map/pallas_call | solution.py:406
  43.7 1.5 %copy.17 = bf16[1,160,256]{2,1,0:T(8,128)(2,1)} copy(bf16[1,160,256]{2,1,0:T(8,128)(2,1)} %bitcast.25) | data formatting | bytes 163840

commit v4 on v3

--- a/solution.py
+++ b/solution.py
@@ -129,6 +129,23 @@
         arrived(piece(i, zz, source), ag_recv.at[i, k], ag_send.at[i, k])
         half = piece(i, zz, source, side * HALF, HALF)
         send(half, half, ag_send.at[i, k + 4], ag_recv.at[i, k + 4], target)
+
+    def ag_cross(i):
+        got = piece(i, zo, y)
+        arrived(got, ag_recv.at[i, 0], ag_send.at[i, 0])
+        for k, target in ((3, up), (4, down)):
+            send(got, got, ag_send.at[i, k], ag_recv.at[i, k], target)
+
+    def ag_over(i, k):
+        got = piece(i, z, y2, k * HALF, HALF)
+        arrived(got, ag_recv.at[i, 5 + k], ag_send.at[i, 5 + k])
+        send(got, got, ag_send.at[i, 7 + k], ag_recv.at[i, 7 + k], across)
+
+    def ag_done_over(i):
+        arrived(piece(i, zo, ym), ag_recv.at[i, 3], ag_send.at[i, 3])
+        arrived(piece(i, zo, yp), ag_recv.at[i, 4], ag_send.at[i, 4])
+        for k in range(2):
+            arrived(piece(i, zo, y2, k * HALF, HALF), ag_recv.at[i, 7 + k], ag_send.at[i, 7 + k])
 
     def ag_done(i):
         arrived(piece(i, zo, y), ag_recv.at[i, 0], ag_send.at[i, 0])
@@ -303,15 +320,15 @@
     @pl.when(branch < 2)
     def _():
         conv_second(0, 0, 0)
-        conv_second(0, 0, 3)
     rs1(0, 0)
     rs1(0, 1)
+    @pl.when(branch < 2)
+    def _():
+        conv_second(0, 0, 3)
+        conv_second(0, 0, 1)
+        conv_second(0, 0, 2)
     rsz(0, 0)
     rsz(0, 1)
-    @pl.when(branch < 2)
-    def _():
-        conv_second(0, 0, 1)
-        conv_second(0, 0, 2)
     ag_relay(2, 1)
     ag_relay(2, 2)
     ag_done(1)
@@ -330,15 +347,15 @@
     @pl.when(branch < 2)
     def _():
         conv_second(1, 0, 0)
-        conv_second(1, 0, 3)
     rs1(1, 0)
     rs1(1, 1)
+    @pl.when(branch < 2)
+    def _():
+        conv_second(1, 0, 3)
+        conv_second(1, 0, 1)
+        conv_second(1, 0, 2)
     rsz(1, 0)
     rsz(1, 1)
-    @pl.when(branch < 2)
-    def _():
-        conv_second(1, 0, 1)
-        conv_second(1, 0, 2)
     rs2(0, 1, 0)
     rs2(0, 1, 1)
     loads["zc"].wait()

time: 45.4 us -> 45.4 us (level)
  no operation moved by 1% of the time
where the time goes in v4:
time: 45.4 us; the launch traced here: 45.2 us
  Pallas kernels  43.7 us (96%)
  local copies, waits for them, and re-layouts  1.53 us (3%)
    pallas_call x1, Pallas kernels, shards(): pl.pallas_call(kernel, out_shape=jax.ShapeDtypeStruct((WIDTH, PIX), BF16)...  43.7 us
    unnamed x1, local copies, waits for them, and re-layouts  1.53 us

profile of v4, /device:TPU:0, one launch (start us, length us, event | category | flops | bytes accessed | tf_op | source)
XLA Modules:
  0.0 45.2 jit_solution(8005299283820696218)
XLA Ops:
  0.0 43.7 %shard_map.145 = bf16[160,256]{1,0:T(8,128)(2,1)} custom-call(s32[1,2]{1,0:T(1,128)} %bitcast.28, s32[1,2]{1,0:T(1,128)} %bitcast.29, bf16[160,256]{1,0:T(8,128)(2,1)} %bitcast.27, bf16[2,160,256]{2,1,0:T(8,128)(2,1)} %bitcast.26, bf16[320,1280]{1,0:T(8,128)(2,1)} %utf.1, bf16[1280,1280]{1,0:T(8,128)(2,1)} %uts.1, bf16[160,1280]{1,0:T(8,128)(2,1)} %bitcast.22, ...), custom_call_target="tpu_custom_call" | custom-call | tf_op jit(solution)/shard_map/pallas_call | solution.py:423
  43.7 1.5 %copy.17 = bf16[1,160,256]{2,1,0:T(8,128)(2,1)} copy(bf16[1,160,256]{2,1,0:T(8,128)(2,1)} %bitcast.25) | data formatting | bytes 163840
